TPU v7x, 32 devices: a whole 2x2x4 slice. The times are simulated.
32 devices in a mesh: tm: 8 (over y, x, core), chan: 4 (over z).
Axes of the slice: x: 2, y: 2, z: 4, core: 2. Of those that a mesh axis runs over, the one named last changes fastest.
Arguments:
- auxiliary: float32 [512, 262144], P('chan', 'tm'), may hold values from -30 to 30
- proofs: float32 [64, 262144], P('chan', 'tm'), may hold values from -12 to 12
Outputs:
- coherence: float32 [512, 64, 4096], P('chan', None, 'tm')
All inputs are finite; a program needn't handle non-finite values.
Results may differ from a plain program's by a relative error of at most 0.00076.
Values may be sent and summed in bfloat16 or wider, within the bound.
A program may use at most 192 MiB of HBM per device.

v0:
```python
import math
import jax
import jax.numpy as jnp
from jax import lax
from jax.sharding import PartitionSpec as P

SEG_LEN = 8192
FACTOR = 64
STRIDE = 4096
BINS = 4096


def shifted(value, axis, by):
    peers = lax.axis_size(axis)
    pairs = [(i, i + by) for i in range(peers) if 0 <= i + by < peers]
    return lax.ppermute(value, axis, pairs)


def angle_table(left_count, right_count, modulus):
    left_index = jnp.arange(left_count, dtype=jnp.int32)
    right_index = jnp.arange(right_count, dtype=jnp.int32)
    product = left_index[:, None] * right_index[None, :] % modulus
    return 2.0 * math.pi / modulus * product.astype(jnp.float32)


def transform_block(windowed):
    row_count = windowed.shape[0]
    second = SEG_LEN // FACTOR
    highest = lax.Precision.HIGHEST
    angle_first = angle_table(FACTOR, FACTOR, FACTOR)
    angle_twist = angle_table(FACTOR, second, SEG_LEN)
    angle_second = angle_table(second, second // 2, second)
    cos_twist = jnp.cos(angle_twist)
    sin_twist = jnp.sin(angle_twist)
    cos_second = jnp.cos(angle_second)
    sin_second = jnp.sin(angle_second)
    shaped = windowed.reshape(row_count, FACTOR, second)
    real_one = jnp.einsum("rpq,pk->rkq", shaped, jnp.cos(angle_first), precision=highest)
    imag_one = -jnp.einsum("rpq,pk->rkq", shaped, jnp.sin(angle_first), precision=highest)
    real_two = real_one * cos_twist + imag_one * sin_twist
    imag_two = imag_one * cos_twist - real_one * sin_twist
    real_out = jnp.einsum("rkq,qm->rmk", real_two, cos_second, precision=highest) + jnp.einsum(
        "rkq,qm->rmk", imag_two, sin_second, precision=highest
    )
    imag_out = jnp.einsum("rkq,qm->rmk", imag_two, cos_second, precision=highest) - jnp.einsum(
        "rkq,qm->rmk", real_two, sin_second, precision=highest
    )
    return (real_out.reshape(row_count, BINS), imag_out.reshape(row_count, BINS))


def transform(windowed):
    row_count = windowed.shape[0]
    block_rows = math.gcd(row_count, 64)
    blocks = windowed.reshape(row_count // block_rows, block_rows, SEG_LEN)
    real_out, imag_out = lax.map(transform_block, blocks)
    return (real_out.reshape(row_count, BINS), imag_out.reshape(row_count, BINS))


def segments_of(signal, seg_count):
    channels = signal.shape[0]
    blocks = signal.reshape(channels, seg_count + 1, STRIDE)
    segments = jnp.concatenate([blocks[:, :-1], blocks[:, 1:]], axis=2)
    position = jnp.arange(SEG_LEN, dtype=jnp.float32)
    window = 0.5 - 0.5 * jnp.cos(2.0 * math.pi * position / SEG_LEN)
    return (segments * window).reshape(channels * seg_count, SEG_LEN)


def channel_totals(local_sums):
    return lax.psum((local_sums[0], local_sums[1]), "tm")


def coherence_block(aux_moved, aux_power, wit_piece):
    left_real = jnp.concatenate([aux_moved[0], aux_moved[1]], axis=1)
    left_imag = jnp.concatenate([aux_moved[1], -aux_moved[0]], axis=1)
    right_side = jnp.concatenate([wit_piece[0], wit_piece[1]], axis=1)
    cross_real = jnp.einsum(
        "csf,wsf->cwf", left_real, right_side, preferred_element_type=jnp.float32
    )
    cross_imag = jnp.einsum(
        "csf,wsf->cwf", left_imag, right_side, preferred_element_type=jnp.float32
    )
    wit_float = wit_piece.astype(jnp.float32)
    wit_power = jnp.sum(wit_float * wit_float, axis=(0, 2))
    return (cross_real * cross_real + cross_imag * cross_imag) / (
        (aux_power[:, None, :] + 1e-06) * (wit_power[None, :, :] + 1e-06)
    )


def per_device(auxiliary, proofs):
    aux_rows = auxiliary.shape[0]
    seg_count = auxiliary.shape[1] // STRIDE
    tm_size = lax.axis_size("tm")
    next_aux, next_wit = shifted((auxiliary[:, :STRIDE], proofs[:, :STRIDE]), "tm", -1)
    signal = jnp.concatenate(
        [
            jnp.concatenate([auxiliary, next_aux], axis=1),
            jnp.concatenate([proofs, next_wit], axis=1),
        ],
        axis=0,
    )
    channels = signal.shape[0]
    local_sums = (jnp.sum(auxiliary, axis=1), jnp.sum(proofs, axis=1))
    total_samples = auxiliary.shape[1] * tm_size
    real_part, imag_part = transform(segments_of(signal, seg_count))
    totals = channel_totals(local_sums)
    channel_means = jnp.concatenate(totals) / total_samples
    bin_index = jnp.arange(BINS, dtype=jnp.int32)
    offset_table = jnp.where(
        bin_index == 0, -0.5 * SEG_LEN, jnp.where(bin_index == 1, 0.25 * SEG_LEN, 0.0)
    ).astype(jnp.float32)
    real_part = real_part + jnp.repeat(channel_means, seg_count)[:, None] * offset_table[None, :]
    spectra = (
        jnp.stack([real_part, imag_part]).astype(jnp.bfloat16).reshape(2, channels, seg_count, BINS)
    )
    aux_spec = spectra[:, :aux_rows]
    wit_spec = spectra[:, aux_rows:]
    aux_moved, wit_moved = (
        lax.all_to_all(aux_spec, "tm", split_axis=3, concat_axis=2, tiled=True),
        lax.all_to_all(wit_spec, "tm", split_axis=3, concat_axis=2, tiled=True),
    )
    kept_segments = seg_count * tm_size - 1
    aux_moved = aux_moved[:, :, :kept_segments]
    wit_moved = wit_moved[:, :, :kept_segments]
    aux_float = aux_moved.astype(jnp.float32)
    aux_power = jnp.sum(aux_float * aux_float, axis=(0, 2))
    return coherence_block(
        aux_moved, aux_power, lax.all_gather(wit_moved, "chan", axis=1, tiled=True)
    )


def solution(mesh):
    return jax.shard_map(
        per_device,
        mesh=mesh,
        in_specs=(P("chan", "tm"), P("chan", "tm")),
        out_specs=P("chan", None, "tm"),
        check_vma=False,
    )
```

profile of v0, /device:TPU:0, one launch (start us, length us, event | category | flops | bytes accessed | tf_op | source)
XLA Modules:
  0.0 1519.9 jit_solution(11121710718804022927)
XLA Ops:
  19.4 28.3 %all-reduce = (f32[16]{0:T(128)S(1)}, f32[128]{0:T(128)S(1)}) all-reduce(f32[16]{0:T(128)S(1)} %reduce_sum.37, f32[128]{0:T(128)S(1)} %reduce_sum.36), channel_id=1, replica_groups=mesh['tm'=8,'chan'=4] {'tm'}, use_global_device_ids=true, to_apply=%region_5.6 | all-reduce | flops 144 | bytes 1152 | tf_op jit(solution)/shard_map/psum | solution.py:69
  47.8 19.2 %maximum_maximum_fusion = f32[144,36864]{1,0:T(8,128)} fusion(f32[16,4096]{1,0:T(8,128)S(1)} %collective-permute-done.1, f32[16,32768]{1,0:T(8,128)S(1)} %copy-done.6, f32[128,4096]{1,0:T(8,128)} %collective-permute-done, f32[128,32768]{1,0:T(8,128)} %param.4), kind=kLoop, calls=%fused_computation.83 | loop fusion | flops 15925248 | bytes 42467328 | tf_op jit(solution)/shard_map/concatenate | solution.py:94
  67.0 23.5 %reshape.121 = f32[144,9,4096]{2,1,0:T(8,128)} reshape(f32[144,36864]{1,0:T(8,128)} %maximum_maximum_fusion) | data formatting | bytes 42467328 | tf_op jit(solution)/shard_map/reshape | solution.py:61
  90.5 32.4 %fusion.86 = (f32[144,8,4096]{2,1,0:T(8,128)}, f32[144,8,4096]{2,1,0:T(8,128)}) fusion(f32[144,9,4096]{2,1,0:T(8,128)} %reshape.121), kind=kLoop, calls=%fused_computation.109 | loop fusion | bytes 75497472 | tf_op jit(solution)/shard_map/slice | solution.py:62
  122.9 24.7 %maximum_multiply_fusion = f32[18,64,8192]{2,1,0:T(8,128)} fusion(f32[18,64,4096]{2,1,0:T(8,128)} %bitcast.103, f32[18,64,4096]{2,1,0:T(8,128)} %bitcast.102, f32[8192]{0:T(1024)S(1)} %multiply_subtract_fusion.3), kind=kLoop, calls=%fused_computation.80 | loop fusion | flops 18874368 | bytes 75530240 | tf_op jit(solution)/shard_map/mul | solution.py:65
  147.7 764.7 %while.15 = (s32[]{:T(128)}, f32[18,64,4096]{2,1,0:T(8,128)}, bf16[18,64,4096]{2,1,0:T(8,128)(2,1)}, f32[18,64,8192]{2,1,0:T(8,128)}, s32[]{:T(128)}) while((s32[]{:T(128)}, f32[18,64,4096]{2,1,0:T(8,128)}, bf16[18,64,4096]{2,1,0:T(8,128)(2,1)}, f32[18,64,8192]{2,1,0:T(8,128)}, s32[]{:T(128)}) %tuple.35), condition=%wide.region_1.0_spmd, body=%wide.region_0.0_spmd.sunk | while | flops 2425782272 | bytes 56426632 | solution.py:55
  232.0 9.2 add_bitcast_fusion.2
  357.0 9.2 add_bitcast_fusion.2
  482.0 9.2 add_bitcast_fusion.2
  924.6 13.7 copy.29
  938.3 18.8 %reshape.127 = bf16[8,2,65536]{2,1,0:T(2,128)(2,1)S(1)} reshape(bf16[4096,2,8,16]{3,2,1,0:T(8,128)(2,1)} %bitcast.104) | data formatting | bytes 4194304
  957.2 31.7 %all_to_all.36 = bf16[8,2,65536]{2,1,0:T(2,128)(2,1)} all-to-all(bf16[8,2,65536]{2,1,0:T(2,128)(2,1)S(1)} %reshape.127), channel_id=1, replica_groups=mesh['tm'=8,'chan'=4] {'tm'}, dimensions={0} | all-to-all | bytes 4194304 | tf_op jit(solution)/shard_map/all_to_all | solution.py:119
  988.8 13.9 reshape.128
  1002.8 17.5 %copy.31 = bf16[2,16,8,8,512]{4,3,2,1,0:T(8,128)(2,1)S(1)} copy(bf16[2,16,8,8,512]{1,3,0,4,2:T(8,128)(2,1)} %bitcast.105) | data formatting | bytes 4194304 | tf_op jit(solution)/shard_map/all_to_all | solution.py:119
  1025.2 15.3 %pad_maximum_fusion = bf16[2,128,8,4096]{3,2,1,0:T(8,128)(2,1)} fusion(bf16[1,144,8,4096]{3,2,1,0:T(8,128)(2,1)} %bitcast.108, bf16[1,144,8,4096]{3,2,1,0:T(8,128)(2,1)} %copy-done.2), kind=kLoop, calls=%fused_computation.85 | loop fusion | flops 8388608 | bytes 35651584 | tf_op jit(solution)/shard_map/stack | solution.py:113
  1040.5 24.3 %copy.33 = bf16[2,128,8,4096]{1,2,0,3:T(8,128)(2,1)} copy(bf16[2,128,8,4096]{3,2,1,0:T(8,128)(2,1)} %pad_maximum_fusion) | data formatting | bytes 33554432 | tf_op jit(solution)/shard_map/slice | solution.py:115
  1070.7 240.2 %all-gather.2.cloned.1.call-done = bf16[2,64,63,512]{2,1,3,0:T(8,128)(2,1)} async-done(((bf16[2,16,63,512]{2,1,3,0:T(8,128)(2,1)}), bf16[2,64,63,512]{2,1,3,0:T(8,128)(2,1)}) %all-gather.2.cloned.1.call-update) | async-done | bytes 8257552 | tf_op jit(solution)/shard_map/all_gather | solution.py:127
  1328.9 25.1 %copy.35 = bf16[2,128,8,8,512]{4,3,2,1,0:T(8,128)(2,1)} copy(bf16[2,128,8,8,512]{1,3,0,4,2:T(8,128)(2,1)} %bitcast.20) | data formatting | bytes 33554432 | tf_op jit(solution)/shard_map/all_to_all | solution.py:118
  1371.0 26.8 %copy.44 = bf16[1,128,63,512]{2,1,3,0:T(8,128)(2,1)} copy(bf16[1,128,63,512]{3,2,1,0:T(8,128)(2,1)} %get-tuple-element.101) | data formatting | bytes 16515072
  1397.8 14.2 bitcast_negate_fusion
  1412.0 26.7 %copy.45 = bf16[1,128,63,512]{2,1,3,0:T(8,128)(2,1)} copy(bf16[1,128,63,512]{3,2,1,0:T(8,128)(2,1)} %get-tuple-element.102) | data formatting | bytes 16515072
  1438.6 26.9 %fusion.74 = f32[512,64,128]{2,1,0:T(8,128)} fusion(bf16[128,63,512]{1,0,2:T(8,128)(2,1)} %bitcast.106, bf16[128,63,512]{1,0,2:T(8,128)(2,1)} %bitcast.101, bf16[64,63,512]{1,0,2:T(8,128)(2,1)} %get-tuple-element.100, bf16[64,63,512]{1,0,2:T(8,128)(2,1)} %get-tuple-element.99), kind=kOutput, calls=%fused_computation.86 | convolution fusion | flops 1106509824 | bytes 41549824 | tf_op jit(solution)/shard_map/csf,wsf->cwf/dot_general | solution.py:76
  1465.5 29.8 %bitcast_divide_fusion = f32[128,64,512]{0,1,2:T(8,128)} fusion(f32[512,64,128]{2,1,0:T(8,128)} %fusion.74, bf16[128,63,512]{1,0,2:T(8,128)(2,1)} %bitcast_negate_fusion, bf16[128,63,512]{1,0,2:T(8,128)(2,1)} %bitcast.107, f32[64,512]{0,1:T(8,128)S(1)} %broadcast_add_fusion, f32[128,512]{0,1:T(8,128)S(1)} %copy.38, ...), kind=kOutput, calls=%fused_computation.94 | convolution fusion | flops 1127481344 | bytes 58720256 | tf_op jit(solution)/shard_map/csf,wsf->cwf/dot_general | solution.py:79
  1495.4 17.5 %copy.39 = f32[128,64,512]{2,1,0:T(8,128)} copy(f32[128,64,512]{0,1,2:T(8,128)} %bitcast_divide_fusion) | data formatting | bytes 33554432 | tf_op jit(solution)/shard_map/div | solution.py:84
  (340 shorter events, 792.0 us)
Async XLA Ops:
  6.5 1304.4 %all-gather.2.cloned.1.call-start = ((), (), s32[]{:S(2)}) async-start(), calls=%async_computation.2 | async-start | bytes 20971520 | tf_op jit(solution)/shard_map/all_gather | solution.py:127
  9.7 38.2 %collective-permute-start = (f32[128,4096]{1,0:T(8,128)}, f32[128,4096]{1,0:T(8,128)}, u32[]{:S(2)}, u32[]{:S(2)}) collective-permute-start(f32[128,4096]{1,0:T(8,128)} %slice.40), channel_id=1, source_target_pairs={{4,0},{8,4},{12,8},{16,12},{20,16},{24,20},{28,24},{5,1},{9,5},{13... | collective-permute-start | bytes 6291464 | tf_op jit(solution)/shard_map/ppermute | solution.py:16
  18.1 29.8 %collective-permute-start.1 = (f32[16,4096]{1,0:T(8,128)S(1)}, f32[16,4096]{1,0:T(8,128)S(1)}, u32[]{:S(2)}, u32[]{:S(2)}) collective-permute-start(f32[16,4096]{1,0:T(8,128)S(1)} %slice.41), channel_id=1, source_target_pairs={{4,0},{8,4},{12,8},{16,12},{20,16},{24,20},{28,24},{5,1},{9,5},{13... | collective-permute-start | bytes 786440 | tf_op jit(solution)/shard_map/ppermute | solution.py:16
  182.6 19.2 %copy-start.4 = (bf16[1,64,4096]{2,1,0:T(8,128)(2,1)S(1)}, bf16[1,64,4096]{2,1,0:T(8,128)(2,1)}, u32[]{:S(2)}) copy-start(bf16[1,64,4096]{2,1,0:T(8,128)(2,1)} %broadcast_in_dim.51) | copy-start | bytes 1572868 | tf_op jit(solution)/shard_map/while
  224.2 19.2 %copy-start.4 = (bf16[1,64,4096]{2,1,0:T(8,128)(2,1)S(1)}, bf16[1,64,4096]{2,1,0:T(8,128)(2,1)}, u32[]{:S(2)}) copy-start(bf16[1,64,4096]{2,1,0:T(8,128)(2,1)} %broadcast_in_dim.51) | copy-start | bytes 1572868 | tf_op jit(solution)/shard_map/while
  265.8 19.2 %copy-start.4 = (bf16[1,64,4096]{2,1,0:T(8,128)(2,1)S(1)}, bf16[1,64,4096]{2,1,0:T(8,128)(2,1)}, u32[]{:S(2)}) copy-start(bf16[1,64,4096]{2,1,0:T(8,128)(2,1)} %broadcast_in_dim.51) | copy-start | bytes 1572868 | tf_op jit(solution)/shard_map/while
  307.5 19.2 %copy-start.4 = (bf16[1,64,4096]{2,1,0:T(8,128)(2,1)S(1)}, bf16[1,64,4096]{2,1,0:T(8,128)(2,1)}, u32[]{:S(2)}) copy-start(bf16[1,64,4096]{2,1,0:T(8,128)(2,1)} %broadcast_in_dim.51) | copy-start | bytes 1572868 | tf_op jit(solution)/shard_map/while
  349.2 19.2 %copy-start.4 = (bf16[1,64,4096]{2,1,0:T(8,128)(2,1)S(1)}, bf16[1,64,4096]{2,1,0:T(8,128)(2,1)}, u32[]{:S(2)}) copy-start(bf16[1,64,4096]{2,1,0:T(8,128)(2,1)} %broadcast_in_dim.51) | copy-start | bytes 1572868 | tf_op jit(solution)/shard_map/while
  390.8 19.2 %copy-start.4 = (bf16[1,64,4096]{2,1,0:T(8,128)(2,1)S(1)}, bf16[1,64,4096]{2,1,0:T(8,128)(2,1)}, u32[]{:S(2)}) copy-start(bf16[1,64,4096]{2,1,0:T(8,128)(2,1)} %broadcast_in_dim.51) | copy-start | bytes 1572868 | tf_op jit(solution)/shard_map/while
  432.5 19.2 %copy-start.4 = (bf16[1,64,4096]{2,1,0:T(8,128)(2,1)S(1)}, bf16[1,64,4096]{2,1,0:T(8,128)(2,1)}, u32[]{:S(2)}) copy-start(bf16[1,64,4096]{2,1,0:T(8,128)(2,1)} %broadcast_in_dim.51) | copy-start | bytes 1572868 | tf_op jit(solution)/shard_map/while
  474.1 19.2 %copy-start.4 = (bf16[1,64,4096]{2,1,0:T(8,128)(2,1)S(1)}, bf16[1,64,4096]{2,1,0:T(8,128)(2,1)}, u32[]{:S(2)}) copy-start(bf16[1,64,4096]{2,1,0:T(8,128)(2,1)} %broadcast_in_dim.51) | copy-start | bytes 1572868 | tf_op jit(solution)/shard_map/while
  515.8 19.2 %copy-start.4 = (bf16[1,64,4096]{2,1,0:T(8,128)(2,1)S(1)}, bf16[1,64,4096]{2,1,0:T(8,128)(2,1)}, u32[]{:S(2)}) copy-start(bf16[1,64,4096]{2,1,0:T(8,128)(2,1)} %broadcast_in_dim.51) | copy-start | bytes 1572868 | tf_op jit(solution)/shard_map/while
  557.5 19.2 %copy-start.4 = (bf16[1,64,4096]{2,1,0:T(8,128)(2,1)S(1)}, bf16[1,64,4096]{2,1,0:T(8,128)(2,1)}, u32[]{:S(2)}) copy-start(bf16[1,64,4096]{2,1,0:T(8,128)(2,1)} %broadcast_in_dim.51) | copy-start | bytes 1572868 | tf_op jit(solution)/shard_map/while
  599.2 19.2 %copy-start.4 = (bf16[1,64,4096]{2,1,0:T(8,128)(2,1)S(1)}, bf16[1,64,4096]{2,1,0:T(8,128)(2,1)}, u32[]{:S(2)}) copy-start(bf16[1,64,4096]{2,1,0:T(8,128)(2,1)} %broadcast_in_dim.51) | copy-start | bytes 1572868 | tf_op jit(solution)/shard_map/while
  640.8 19.2 %copy-start.4 = (bf16[1,64,4096]{2,1,0:T(8,128)(2,1)S(1)}, bf16[1,64,4096]{2,1,0:T(8,128)(2,1)}, u32[]{:S(2)}) copy-start(bf16[1,64,4096]{2,1,0:T(8,128)(2,1)} %broadcast_in_dim.51) | copy-start | bytes 1572868 | tf_op jit(solution)/shard_map/while
  682.5 19.2 %copy-start.4 = (bf16[1,64,4096]{2,1,0:T(8,128)(2,1)S(1)}, bf16[1,64,4096]{2,1,0:T(8,128)(2,1)}, u32[]{:S(2)}) copy-start(bf16[1,64,4096]{2,1,0:T(8,128)(2,1)} %broadcast_in_dim.51) | copy-start | bytes 1572868 | tf_op jit(solution)/shard_map/while
  724.1 19.2 %copy-start.4 = (bf16[1,64,4096]{2,1,0:T(8,128)(2,1)S(1)}, bf16[1,64,4096]{2,1,0:T(8,128)(2,1)}, u32[]{:S(2)}) copy-start(bf16[1,64,4096]{2,1,0:T(8,128)(2,1)} %broadcast_in_dim.51) | copy-start | bytes 1572868 | tf_op jit(solution)/shard_map/while
  765.8 19.2 %copy-start.4 = (bf16[1,64,4096]{2,1,0:T(8,128)(2,1)S(1)}, bf16[1,64,4096]{2,1,0:T(8,128)(2,1)}, u32[]{:S(2)}) copy-start(bf16[1,64,4096]{2,1,0:T(8,128)(2,1)} %broadcast_in_dim.51) | copy-start | bytes 1572868 | tf_op jit(solution)/shard_map/while
  807.5 19.2 %copy-start.4 = (bf16[1,64,4096]{2,1,0:T(8,128)(2,1)S(1)}, bf16[1,64,4096]{2,1,0:T(8,128)(2,1)}, u32[]{:S(2)}) copy-start(bf16[1,64,4096]{2,1,0:T(8,128)(2,1)} %broadcast_in_dim.51) | copy-start | bytes 1572868 | tf_op jit(solution)/shard_map/while
  849.2 19.2 %copy-start.4 = (bf16[1,64,4096]{2,1,0:T(8,128)(2,1)S(1)}, bf16[1,64,4096]{2,1,0:T(8,128)(2,1)}, u32[]{:S(2)}) copy-start(bf16[1,64,4096]{2,1,0:T(8,128)(2,1)} %broadcast_in_dim.51) | copy-start | bytes 1572868 | tf_op jit(solution)/shard_map/while
  890.9 19.2 %copy-start.4 = (bf16[1,64,4096]{2,1,0:T(8,128)(2,1)S(1)}, bf16[1,64,4096]{2,1,0:T(8,128)(2,1)}, u32[]{:S(2)}) copy-start(bf16[1,64,4096]{2,1,0:T(8,128)(2,1)} %broadcast_in_dim.51) | copy-start | bytes 1572868 | tf_op jit(solution)/shard_map/while
  912.4 12.0 copy-start.5
  1064.8 264.1 %all-to-all-start.1 = ((bf16[2,128,8,4096]{1,2,0,3:T(8,128)(2,1)}), bf16[2,128,8,4096]{1,2,0,3:T(8,128)(2,1)}, u32[]{:S(2)}, u32[]{:S(2)}) async-start(bf16[2,128,8,4096]{1,2,0,3:T(8,128)(2,1)} %copy.33), calls=%async_computation.1 | async-start | bytes 33554432 | tf_op jit(solution)/shard_map/all_to_all | solution.py:118
  1311.0 10.7 copy-start.3
  (21 other events, 134.1 us)
Sparse Core Ops, SparseCore 0:
  1025.3 285.5 all-gather.1
where the time goes:
time: 1530 us; the launch traced here: 1520 us
  matrix products  663 us (43%)
  local copies, waits for them, and re-layouts  411 us (27%)
  waiting for transfers between devices  240 us (16%)
  other arithmetic  108 us (7%)
  blocking collectives  59.9 us (4%)
  loops' own time  15.9 us (1%)
    all_gather x1, waiting for transfers between devices, per_device(): lax.all_gather(wit_moved, 'chan', axis=1, tiled=True)  240 us
    dot_general x18, matrix products, transform_block(): jnp.einsum('rkq,qm->rmk', real_two, cos_second, precision=highest)  166 us
    dot_general x18, matrix products, transform_block(): jnp.einsum('rkq,qm->rmk', imag_two, sin_second, precision=highest)  141 us
    dot_general x18, matrix products, transform_block(): jnp.einsum('rkq,qm->rmk', real_two, sin_second, precision=highest)  113 us
    dot_general x18, matrix products, transform_block(): jnp.einsum('rkq,qm->rmk', imag_two, cos_second, precision=highest)  112 us
    unnamed x15, local copies, waits for them, and re-layouts  100 us
    broadcast_in_dim x36, local copies, waits for them, and re-layouts, transform(): real_out, imag_out = lax.map(transform_block, blocks)  67.4 us
    while x108, local copies, waits for them, and re-layouts  38.3 us
  transfers between devices with their start and end apart: 4, of which 1 were waited for; matrix products, arithmetic and copies ran while one was open for 4% of the time, Pallas kernels for 0%

commit v1 on v0

--- a/solution.py
+++ b/solution.py
@@ -124,7 +124,7 @@
     aux_float = aux_moved.astype(jnp.float32)
     aux_power = jnp.sum(aux_float * aux_float, axis=(0, 2))
     return coherence_block(
-        aux_moved, aux_power, lax.all_gather(wit_moved, "chan", axis=1, tiled=True)
+        aux_moved, aux_power, jnp.concatenate(lax.all_gather(wit_moved, "chan"), axis=1)
     )
 
 

time: 1530 us -> 1440 us (0.941)
  waiting for transfers between devices: 240 us -> 149 us
  local copies, waits for them, and re-layouts: 411 us -> 461 us
  blocking collectives: 59.9 us -> 27.3 us
    all_gather x1, waiting for transfers between devices: 240 us -> 149 us  [per_device(): lax.all_gather(wit_moved, 'chan')]
    slice x0 -> x4, local copies, waits for them, and re-layouts: none -> 38.2 us  [the longest x3 36.7 us: coherence_block(): right_side = jnp.concatenate([wit_piece[0], wit_piece[1]], axis=1)]
    all_to_all x1 -> x0, blocking collectives: 31.7 us -> none  [per_device(): lax.all_to_all(wit_spec, 'tm', split_axis=3, concat_axis=2, tiled=True)]
    dynamic_update_slice x36, local copies, waits for them, and re-layouts: 34.4 us -> 53.2 us  [transform(): real_out, imag_out = lax.map(transform_block, blocks)]
    unnamed x15 -> x18, local copies, waits for them, and re-layouts: 100 us -> 92.7 us
    while x108 -> x72, local copies, waits for them, and re-layouts: 38.3 us -> 38.1 us
  transfers between devices with their start and end apart: 4 -> 5, of which waited for: 1 -> 1; matrix products, arithmetic and copies ran while one was open for 4% -> 8% of each run, Pallas kernels for 0% -> 0%
where the time goes in v1:
time: 1440 us; the launch traced here: 1430 us
  matrix products  661 us (46%)
  local copies, waits for them, and re-layouts  461 us (32%)
  waiting for transfers between devices  149 us (10%)
  other arithmetic  101 us (7%)
  blocking collectives  27.3 us (2%)
    dot_general x18, matrix products, transform_block(): jnp.einsum('rkq,qm->rmk', real_two, cos_second, precision=highest)  165 us
    all_gather x1, waiting for transfers between devices, per_device(): lax.all_gather(wit_moved, 'chan')  149 us
    dot_general x18, matrix products, transform_block(): jnp.einsum('rkq,qm->rmk', imag_two, sin_second, precision=highest)  140 us
    dot_general x18, matrix products, transform_block(): jnp.einsum('rkq,qm->rmk', real_two, sin_second, precision=highest)  113 us
    dot_general x18, matrix products, transform_block(): jnp.einsum('rkq,qm->rmk', imag_two, cos_second, precision=highest)  112 us
    unnamed x18, local copies, waits for them, and re-layouts  92.7 us
    broadcast_in_dim x36, local copies, waits for them, and re-layouts, transform(): real_out, imag_out = lax.map(transform_block, blocks)  68.1 us
    dynamic_update_slice x36, local copies, waits for them, and re-layouts, transform(): real_out, imag_out = lax.map(transform_block, blocks)  53.2 us
  transfers between devices with their start and end apart: 5, of which 1 were waited for; matrix products, arithmetic and copies ran while one was open for 8% of the time, Pallas kernels for 0%

profile of v1, /device:TPU:0, one launch (start us, length us, event | category | flops | bytes accessed | tf_op | source)
XLA Modules:
  0.0 1428.4 jit_solution(5971478277093336269)
XLA Ops:
  20.3 27.3 %all-reduce = (f32[16]{0:T(128)S(1)}, f32[128]{0:T(128)S(1)}) all-reduce(f32[16]{0:T(128)S(1)} %reduce_sum.37, f32[128]{0:T(128)S(1)} %reduce_sum.36), channel_id=1, replica_groups=mesh['tm'=8,'chan'=4] {'tm'}, use_global_device_ids=true, to_apply=%region_5.6 | all-reduce | flops 144 | bytes 1152 | tf_op jit(solution)/shard_map/psum | solution.py:69
  47.8 19.1 %maximum_maximum_fusion = f32[144,36864]{1,0:T(8,128)} fusion(f32[16,4096]{1,0:T(8,128)S(1)} %collective-permute-done.1, f32[16,32768]{1,0:T(8,128)S(1)} %copy-done.3, f32[128,4096]{1,0:T(8,128)} %collective-permute-done, f32[128,32768]{1,0:T(8,128)} %param.4), kind=kLoop, calls=%fused_computation.82 | loop fusion | flops 15925248 | bytes 42467328 | tf_op jit(solution)/shard_map/concatenate | solution.py:94
  67.0 23.5 %reshape.135 = f32[144,9,4096]{2,1,0:T(8,128)} reshape(f32[144,36864]{1,0:T(8,128)} %maximum_maximum_fusion) | data formatting | bytes 42467328 | tf_op jit(solution)/shard_map/reshape | solution.py:61
  90.5 32.4 %fusion.86 = (f32[144,8,4096]{2,1,0:T(8,128)}, f32[144,8,4096]{2,1,0:T(8,128)}) fusion(f32[144,9,4096]{2,1,0:T(8,128)} %reshape.135), kind=kLoop, calls=%fused_computation.107 | loop fusion | bytes 75497472 | tf_op jit(solution)/shard_map/slice | solution.py:62
  122.9 24.7 %maximum_multiply_fusion = f32[18,64,8192]{2,1,0:T(8,128)} fusion(f32[18,64,4096]{2,1,0:T(8,128)} %bitcast.105, f32[18,64,4096]{2,1,0:T(8,128)} %bitcast.104, f32[8192]{0:T(1024)S(1)} %multiply_subtract_fusion.3), kind=kLoop, calls=%fused_computation.80 | loop fusion | flops 18874368 | bytes 75530240 | tf_op jit(solution)/shard_map/mul | solution.py:65
  147.6 768.6 %while.15 = (s32[]{:T(128)}, f32[18,64,4096]{2,1,0:T(8,128)}, bf16[18,64,4096]{2,1,0:T(8,128)(2,1)}, f32[18,64,8192]{2,1,0:T(8,128)}, s32[]{:T(128)}) while((s32[]{:T(128)}, f32[18,64,4096]{2,1,0:T(8,128)}, bf16[18,64,4096]{2,1,0:T(8,128)(2,1)}, f32[18,64,8192]{2,1,0:T(8,128)}, s32[]{:T(128)}) %tuple.35), condition=%wide.region_1.0_spmd, body=%wide.region_0.0_spmd.sunk | while | flops 2425782272 | bytes 54330460 | solution.py:55
  476.7 9.2 add_bitcast_fusion.2
  928.3 13.7 copy.33
  942.1 19.6 %reshape.143 = bf16[8,2,65536]{2,1,0:T(2,128)(2,1)} reshape(bf16[4096,2,8,16]{3,2,1,0:T(8,128)(2,1)} %bitcast.106) | data formatting | bytes 4194304
  966.8 14.8 %pad_maximum_fusion = bf16[2,128,8,4096]{3,2,1,0:T(8,128)(2,1)} fusion(bf16[1,144,8,4096]{3,2,1,0:T(8,128)(2,1)} %bitcast.110, bf16[1,144,8,4096]{3,2,1,0:T(8,128)(2,1)} %copy-done.1), kind=kLoop, calls=%fused_computation.84 | loop fusion | flops 8388608 | bytes 35651584 | tf_op jit(solution)/shard_map/stack | solution.py:113
  981.6 24.1 %copy.37 = bf16[2,128,8,4096]{1,2,0,3:T(8,128)(2,1)} copy(bf16[2,128,8,4096]{3,2,1,0:T(8,128)(2,1)} %pad_maximum_fusion) | data formatting | bytes 33554432 | tf_op jit(solution)/shard_map/slice | solution.py:115
  1011.4 13.2 reshape.144
  1024.7 16.0 %copy.34 = bf16[2,16,8,8,512]{4,1,3,2,0:T(8,128)(2,1)S(1)} copy(bf16[2,16,8,8,512]{1,3,0,4,2:T(8,128)(2,1)} %bitcast.107) | data formatting | bytes 4194304 | tf_op jit(solution)/shard_map/all_to_all | solution.py:119
  1042.2 149.3 %all-gather.3.cloned.1.call-done = bf16[8,16,63,512]{3,1,2,0:T(8,128)(2,1)} async-done(((bf16[2,16,63,512]{3,1,2,0:T(8,128)(2,1)}), bf16[8,16,63,512]{3,1,2,0:T(8,128)(2,1)}) %all-gather.3.cloned.1.call-update) | async-done | bytes 8257552 | tf_op jit(solution)/shard_map/all_gather | solution.py:127
  1197.5 15.3 %copy.35 = bf16[1,4,16,63,512]{3,2,1,4,0:T(8,128)(2,1)} copy(bf16[1,4,16,63,512]{4,2,3,0,1:T(8,128)(2,1)} %get-tuple-element.101) | data formatting | bytes 8257536 | tf_op jit(solution)/shard_map/slice | solution.py:75
  1212.9 15.4 %copy.36 = bf16[1,4,16,63,512]{3,2,1,4,0:T(8,128)(2,1)} copy(bf16[1,4,16,63,512]{4,2,3,0,1:T(8,128)(2,1)} %get-tuple-element.102) | data formatting | bytes 8257536 | tf_op jit(solution)/shard_map/slice | solution.py:75
  1233.7 25.2 %copy.39 = bf16[2,128,8,8,512]{4,3,2,1,0:T(8,128)(2,1)} copy(bf16[2,128,8,8,512]{1,3,0,4,2:T(8,128)(2,1)} %bitcast.22) | data formatting | bytes 33554432 | tf_op jit(solution)/shard_map/all_to_all | solution.py:118
  1258.9 13.6 fusion.87
  1279.4 26.8 %copy.46 = bf16[1,128,63,512]{2,1,3,0:T(8,128)(2,1)} copy(bf16[1,128,63,512]{3,2,1,0:T(8,128)(2,1)} %get-tuple-element.99) | data formatting | bytes 16515072
  1306.2 26.7 %copy.47 = bf16[1,128,63,512]{2,1,3,0:T(8,128)(2,1)} copy(bf16[1,128,63,512]{3,2,1,0:T(8,128)(2,1)} %get-tuple-element.100) | data formatting | bytes 16515072
  1332.8 14.3 %bitcast_negate_fusion = bf16[128,63,512]{1,0,2:T(8,128)(2,1)} fusion(bf16[1,128,63,512]{2,1,3,0:T(8,128)(2,1)} %copy.46), kind=kLoop, calls=%fused_computation.106 | loop fusion | flops 4128768 | bytes 16515072 | tf_op jit(solution)/shard_map/neg | solution.py:74
  1347.4 26.9 %fusion.74 = f32[512,64,128]{2,1,0:T(8,128)} fusion(bf16[128,63,512]{1,0,2:T(8,128)(2,1)} %bitcast.108, bf16[128,63,512]{1,0,2:T(8,128)(2,1)} %bitcast.103, bf16[64,63,512]{1,0,2:T(8,128)(2,1)} %bitcast.114, bf16[64,63,512]{1,0,2:T(8,128)(2,1)} %bitcast.112), kind=kOutput, calls=%fused_computation.85 | convolution fusion | flops 1106509824 | bytes 41549824 | tf_op jit(solution)/shard_map/csf,wsf->cwf/dot_general | solution.py:76
  1374.3 29.6 %bitcast_divide_fusion = f32[128,64,512]{0,1,2:T(8,128)} fusion(f32[512,64,128]{2,1,0:T(8,128)} %fusion.74, bf16[128,63,512]{1,0,2:T(8,128)(2,1)} %bitcast_negate_fusion, bf16[128,63,512]{1,0,2:T(8,128)(2,1)} %bitcast.109, f32[64,512]{0,1:T(8,128)S(1)} %copy.43, f32[128,512]{0,1:T(8,128)S(1)} %copy.42, bf16[64,63,512]{1,0,2:T(8,128)(2,1)} %bitcast.115, ...), kind=kOutput, calls=%fused_computation.93 | convolution fusion | flops 1127481344 | bytes 58720256 | tf_op jit(solution)/shard_map/csf,wsf->cwf/dot_general | solution.py:79
  1403.9 17.5 %copy.44 = f32[128,64,512]{2,1,0:T(8,128)} copy(f32[128,64,512]{0,1,2:T(8,128)} %bitcast_divide_fusion) | data formatting | bytes 33554432 | tf_op jit(solution)/shard_map/div | solution.py:84
  (313 shorter events, 814.7 us)
Async XLA Ops:
  9.6 9.0 copy-start.3
  9.6 38.2 %collective-permute-start = (f32[128,4096]{1,0:T(8,128)}, f32[128,4096]{1,0:T(8,128)}, u32[]{:S(2)}, u32[]{:S(2)}) collective-permute-start(f32[128,4096]{1,0:T(8,128)} %slice.42), channel_id=1, source_target_pairs={{4,0},{8,4},{12,8},{16,12},{20,16},{24,20},{28,24},{5,1},{9,5},{13... | collective-permute-start | bytes 6291464 | tf_op jit(solution)/shard_map/ppermute | solution.py:16
  19.0 28.8 %collective-permute-start.1 = (f32[16,4096]{1,0:T(8,128)S(1)}, f32[16,4096]{1,0:T(8,128)S(1)}, u32[]{:S(2)}, u32[]{:S(2)}) collective-permute-start(f32[16,4096]{1,0:T(8,128)S(1)} %slice.43), channel_id=1, source_target_pairs={{4,0},{8,4},{12,8},{16,12},{20,16},{24,20},{28,24},{5,1},{9,5},{13... | collective-permute-start | bytes 786440 | tf_op jit(solution)/shard_map/ppermute | solution.py:16
  196.8 6.4 copy-start
  282.1 6.4 copy-start
  367.5 6.4 copy-start
  410.1 6.4 copy-start
  452.8 6.4 copy-start
  495.4 6.4 copy-start
  538.1 6.4 copy-start
  580.7 6.4 copy-start
  666.1 6.4 copy-start
  708.7 6.4 copy-start
  751.4 6.4 copy-start
  794.0 6.4 copy-start
  836.8 6.4 copy-start
  916.2 11.9 copy-start.2
  961.6 44.0 %all-to-all-start = ((bf16[8,2,65536]{2,1,0:T(2,128)(2,1)}), bf16[8,2,65536]{2,1,0:T(2,128)(2,1)S(1)}, u32[]{:S(2)}, u32[]{:S(2)}) async-start(bf16[8,2,65536]{2,1,0:T(2,128)(2,1)} %reshape.143), calls=%async_computation | async-start | bytes 4194304 | tf_op jit(solution)/shard_map/all_to_all | solution.py:119
  1005.7 228.1 %all-to-all-start.1 = ((bf16[2,128,8,4096]{1,2,0,3:T(8,128)(2,1)}), bf16[2,128,8,4096]{1,2,0,3:T(8,128)(2,1)}, u32[]{:S(2)}, u32[]{:S(2)}) async-start(bf16[2,128,8,4096]{1,2,0,3:T(8,128)(2,1)} %copy.37), calls=%async_computation.1 | async-start | bytes 33554432 | tf_op jit(solution)/shard_map/all_to_all | solution.py:118
  1011.4 180.1 %all-gather.3.cloned.1.call-start = ((), (), s32[]{:S(2)}) async-start(), calls=%async_computation.2 | async-start | bytes 10321920 | tf_op jit(solution)/shard_map/all_gather | solution.py:127
  1258.9 13.6 slice-start
  1258.9 13.6 slice-start.1
  1258.9 15.3 %slice-start.2 = ((s8[16777216]{0:T(1024)(128)(4,1)}), s8[4194304]{0:T(1024)(128)(4,1)S(1)}, s32[]{:S(2)}) async-start(s8[16777216]{0:T(1024)(128)(4,1)} %bitcast.100), calls=%async_computation.5 | async-start | bytes 8388608
  1258.9 16.5 %slice-start.3 = ((s8[16777216]{0:T(1024)(128)(4,1)}), s8[4194304]{0:T(1024)(128)(4,1)S(1)}, s32[]{:S(2)}) async-start(s8[16777216]{0:T(1024)(128)(4,1)} %bitcast.100), calls=%async_computation.6 | async-start | bytes 8388608
  (6 other events, 35.3 us)
Sparse Core Ops, SparseCore 0:
  1042.3 149.1 all-gather.2
